TPU v7x, 256 devices: a whole 4x4x8 slice. The times are simulated.
256 devices in a mesh: img: 64 (over z, y, core), rep: 4 (over x).
Axes of the slice: x: 4, y: 4, z: 8, core: 2. Of those that a mesh axis runs over, the one named last changes fastest.
Arguments:
- descriptors: bfloat16 [128, 256, 1024], P('img', 'rep'), may hold values from -0.5 to 0.5
- cell_counts: int32 [128, 256], P('img', 'rep'), may hold values from 1 to 8
- pair_images: int32 [4096, 2], P('img'), may hold values from 0 to 127, as said below
- query_cells: int32 [4096, 16], P('img'), may hold values from 0 to 255
- cand_cells: int32 [4096, 4, 16], P('img', 'rep'), may hold values from 0 to 255, as said below
- cand_counts: int32 [4096, 4], P('img', 'rep'), may hold values from 8 to 16, as said below
Outputs:
- matches: float32 [4096, 2, 128], P('img')
- image_score: float32 [128], P('img')
Inputs may be any that keep to these rules, and one draw needn't show every extreme that they name: `pair_images`: the pairs are numbered by blocks of 64: pair k * 64 + j has its first image among images k * 2 to k * 2 + 1 and its second among images j * 2 to j * 2 + 1; the two images of a pair differ. cand_cells[p, r, s] lies in quarter r, between r * 64 and r * 64 + 63; cells may repeat. `cand_counts`: every count is 8 or 16, and every draw holds at least one count of 16.
All inputs are finite; a program needn't handle non-finite values.
Results may differ from a plain program's by a relative error of at most 0.0003.
Values may be sent and summed in bfloat16 or wider, within the bound.
No kernel may reach another device: no remote copies, remote signals or barrier semaphores. Data moves between devices by JAX's collectives and lax.ppermute only.
A program may use at most 64 MiB of HBM per device.

v0:
```python
import math

import jax
import jax.numpy as jnp
from jax import lax
from jax.sharding import PartitionSpec as P

DESC = 128
KP = 8


distant = 1000000000.0
group_size = 8


def in_one_piece(arrays, axis, dim, along):
    widths = [math.prod(a.shape[along:]) for a in arrays]
    both = jnp.concatenate(
        [a.reshape(*a.shape[:along], w) for a, w in zip(arrays, widths)], axis=along
    )
    out = lax.all_gather(both, axis, axis=dim, tiled=True)
    parts = jnp.split(out, [sum(widths[:k]) for k in range(1, len(widths))], axis=along)
    return tuple((b.reshape(*out.shape[:along], *a.shape[along:]) for a, b in zip(arrays, parts)))


def in_one_piece_2(arrays, axis, split_dim, concat_dim, along):
    columns = [a.reshape(*a.shape[:along], -1) for a in arrays]
    both = jnp.concatenate(columns, axis=along)
    out, at, gathered = (
        lax.all_to_all(both, axis, split_axis=split_dim, concat_axis=concat_dim, tiled=True),
        0,
        [],
    )
    for a, column in zip(arrays, columns):
        slab = out[..., at : at + column.shape[along]]
        gathered.append(slab.reshape(*slab.shape[:along], *a.shape[along:]))
        at += column.shape[along]
    return tuple(gathered)


def from_everyone(shard, axis):
    copies = jnp.broadcast_to(shard, (lax.axis_size(axis), *shard.shape))
    return lax.all_to_all(copies, axis, split_axis=0, concat_axis=0, tiled=True)


def all_in_one(shard, axis):
    leaves = jax.tree.leaves(shard)
    sequence = sorted(range(len(leaves)), key=lambda k: -leaves[k].size)
    width = (1, *leaves[sequence[0]].shape)[-1]
    lines = [
        jnp.pad(leaves[k].reshape(-1), (0, -leaves[k].size % width)).reshape(-1, width)
        for k in sequence
    ]
    both, at, found = (from_everyone(jnp.concatenate(lines), axis), 0, {})
    for k, line in zip(sequence, lines):
        slab = both[:, at : at + len(line)].reshape(len(both), -1)
        found[k] = slab[:, : leaves[k].size].reshape(-1, *leaves[k].shape)
        at += len(line)
    numbers = iter(range(len(leaves)))
    return jax.tree.map(lambda _: found[next(numbers)], shard)


def joined_by_halves(pieces, combine):
    while len(jax.tree.leaves(pieces)[0]) > 1:
        pieces = jax.vmap(combine)(
            *(jax.tree.map(lambda part: part[side::2], pieces) for side in (0, 1))
        )
    return jax.tree.map(lambda part: part[0], pieces)


def combined_all(shard, axis, combine):
    pieces = all_in_one(shard, axis)
    return joined_by_halves(pieces, combine)


def nearest(queries, blocks, block_counts, live_cells):
    pairs = queries.shape[0]
    slots = blocks.shape[1]
    cands = blocks.reshape(pairs, slots * KP, DESC)
    cell_live = jnp.arange(slots, dtype=jnp.int32)[None, :] < live_cells[:, None]
    slot_live = (
        jnp.arange(KP, dtype=jnp.float32)[None, None, :]
        < block_counts.astype(jnp.float32)[:, :, None]
    )
    clive = (cell_live[:, :, None] & slot_live).reshape(pairs, slots * KP)
    groups = pairs // group_size

    def one_group(packed):
        query_part, cand_part, live_part = packed
        qwide = query_part.astype(jnp.float32)
        cwide = cand_part.astype(jnp.float32)
        qnorm = jnp.sum(qwide * qwide, axis=2)
        cnorm = jnp.sum(cwide * cwide, axis=2)
        inner = jnp.einsum(
            "pqd,pcd->pqc", query_part, cand_part, preferred_element_type=jnp.float32
        )
        dist = qnorm[:, :, None] + cnorm[:, None, :] - 2.0 * inner
        dist = jnp.where(live_part[:, None, :], dist, jnp.float32(distant))
        lowest = -lax.top_k(-dist, 2)[0]
        return (lowest[..., 0], lowest[..., 1])

    packed = (
        queries.reshape(groups, group_size, -1, DESC),
        cands.reshape(groups, group_size, -1, DESC),
        clive.reshape(groups, group_size, -1),
    )
    best, runner = lax.map(one_group, packed)
    return (best.reshape(pairs, -1), runner.reshape(pairs, -1))


def keep_two(left, right):
    low = jnp.minimum(left[0], right[0])
    high = jnp.minimum(jnp.maximum(left[0], right[0]), jnp.minimum(left[1], right[1]))
    return (low, high)


def on_device(descriptors, cell_counts, pair_images, query_cells, cand_cells, cand_counts):
    img_dev, share, width = descriptors.shape
    peers = lax.axis_size("img")
    whole, whole_counts = in_one_piece((descriptors, cell_counts.astype(jnp.bfloat16)), "rep", 1, 2)
    cells = whole.shape[1]
    first_local = pair_images[:, 0] % img_dev
    second_local = pair_images[:, 1] % img_dev
    query_rows = (first_local[:, None] * cells + query_cells).reshape(-1)
    queries = jnp.take(whole.reshape(img_dev * cells, width), query_rows, axis=0).reshape(
        peers, -1, DESC
    )
    query_counts = jnp.take(whole_counts.reshape(img_dev * cells), query_rows).reshape(peers, -1)
    qlive = (
        jnp.arange(KP, dtype=jnp.float32)[None, None, :]
        < query_counts.astype(jnp.float32)[:, :, None]
    ).reshape(peers, -1)
    lists = cand_cells[:, 0, :]
    live_cells = cand_counts[:, 0]
    local_rows = descriptors.reshape(img_dev * share, width)
    local_counts = cell_counts.reshape(img_dev * share)
    asked, asked_image = in_one_piece_2((lists, second_local), "img", 0, 0, 1)
    rows = (asked_image[:, None] * share + asked % share).reshape(-1)
    blocks = jnp.take(local_rows, rows, axis=0).reshape(peers, -1, width)
    block_counts = jnp.take(local_counts, rows).reshape(peers, -1).astype(jnp.bfloat16)
    blocks, block_counts = in_one_piece_2((blocks, block_counts), "img", 0, 0, 2)
    best, runner = nearest(queries, blocks, block_counts, live_cells)
    best, runner = combined_all((best, runner), "rep", keep_two)
    best = jnp.where(qlive, best, jnp.float32(0.0))
    runner = jnp.where(qlive, runner, jnp.float32(0.0))
    matches = jnp.stack([best, runner], axis=1)
    margin = jnp.where(qlive, (runner - best) / (runner + 1.0), jnp.float32(0.0))
    score = jnp.sum(margin, axis=1) / jnp.sum(qlive.astype(jnp.float32), axis=1)
    arrived = lax.all_to_all(score, "img", split_axis=0, concat_axis=0, tiled=True)
    image_ids = jnp.arange(img_dev, dtype=jnp.int32)
    own_part = jnp.sum(
        jnp.where(first_local[:, None] == image_ids[None, :], score[:, None], jnp.float32(0.0)),
        axis=0,
    )
    other_part = jnp.sum(
        jnp.where(asked_image[:, None] == image_ids[None, :], arrived[:, None], jnp.float32(0.0)),
        axis=0,
    )
    return (matches, own_part + other_part)


def solution(mesh):
    in_specs = (
        P("img", "rep", None),
        P("img", "rep"),
        P("img", None),
        P("img", None),
        P("img", "rep", None),
        P("img", "rep"),
    )
    out_specs = (P("img", None, None), P("img"))
    return jax.shard_map(
        on_device, mesh=mesh, in_specs=in_specs, out_specs=out_specs, check_vma=False
    )
```

profile of v0, /device:TPU:1, one launch (start us, length us, event | category | flops | bytes accessed | tf_op | source)
XLA Modules:
  0.0 281.2 jit_solution(8775535140133562073)
XLA Ops:
  9.3 13.1 %all-to-all-start = ((s32[64,1,17]{2,1,0:T(1,128)}), s32[64,1,17]{2,1,0:T(1,128)S(1)}, u32[]{:S(2)}, u32[]{:S(2)}) async-start(s32[64,1,17]{2,1,0:T(1,128)} %bitcast.9), calls=%async_computation | async-start | bytes 65536 | tf_op jit(solution)/shard_map/all_to_all | solution.py:30
  23.3 8.6 %all-to-all-done = s32[64,1,17]{2,1,0:T(1,128)S(1)} async-done(((s32[64,1,17]{2,1,0:T(1,128)}), s32[64,1,17]{2,1,0:T(1,128)S(1)}, u32[]{:S(2)}, u32[]{:S(2)}) %all-to-all-start) | async-done | bytes 4384 | tf_op jit(solution)/shard_map/all_to_all | solution.py:30
  32.1 6.6 %gather_fusion.2 = s32[1024]{0:T(1024)S(1)} fusion(s32[128]{0:T(128)S(1)} %reshape.306, s32[1024]{0:T(1024)S(1)} %broadcast_clamp_fusion), kind=kCustom, calls=%fused_computation.2 | custom fusion | bytes 12288 | tf_op jit(solution)/shard_map/jit(_take)/gather | solution.py:140
  39.2 4.1 %gather_fusion.1 = bf16[1024,1024]{1,0:T(8,128)(2,1)S(1)} fusion(bf16[128,1024]{1,0:T(8,128)(2,1)S(1)} %bitcast.93, s32[1024]{0:T(1024)S(1)} %broadcast_clamp_fusion), kind=kCustom, calls=%fused_computation.1 | custom fusion | bytes 4198400 | tf_op jit(solution)/shard_map/jit(_take)/gather | solution.py:139
  45.3 5.7 %all-to-all-start.1 = ((bf16[64,16,1025]{2,1,0:T(8,128)(2,1)}), bf16[64,16,1025]{2,1,0:T(8,128)(2,1)}, u32[]{:S(2)}, u32[]{:S(2)}) async-start(bf16[64,16,1025]{2,1,0:T(8,128)(2,1)} %pad_maximum_fusion), calls=%async_computation.1 | async-start | bytes 4718592 | tf_op jit(solution)/shard_map/all_to_all | solution.py:30
  53.4 26.6 %all-gather.2.cloned.1.call-done = bf16[2,256,1025]{2,1,0:T(8,128)(2,1)} async-done(((bf16[2,64,1025]{2,1,0:T(8,128)(2,1)}), bf16[2,256,1025]{2,1,0:T(8,128)(2,1)}) %all-gather.2.cloned.1.call-update) | async-done | bytes 1049616 | tf_op jit(solution)/shard_map/all_gather | solution.py:21
  81.0 6.8 %gather_fusion = bf16[1024]{0:T(1024)(128)(2,1)S(1)} fusion(bf16[512]{0:T(512)(128)(2,1)S(1)} %bitcast.92, s32[1024]{0:T(1024)S(1)} %broadcast_clamp_fusion.1), kind=kCustom, calls=%fused_computation | custom fusion | bytes 8192 | tf_op jit(solution)/shard_map/jit(_take)/gather | solution.py:128
  88.0 4.1 %gather_fusion.3 = bf16[1024,1024]{1,0:T(8,128)(2,1)S(1)} fusion(bf16[512,1024]{1,0:T(8,128)(2,1)S(1)} %bitcast.94, s32[1024]{0:T(1024)S(1)} %broadcast_clamp_fusion.1), kind=kCustom, calls=%fused_computation.3 | custom fusion | bytes 4198400 | tf_op jit(solution)/shard_map/jit(_take)/gather | solution.py:125
  97.6 9.0 %all-to-all-done.1 = bf16[64,16,1025]{2,1,0:T(8,128)(2,1)} async-done(((bf16[64,16,1025]{2,1,0:T(8,128)(2,1)}), bf16[64,16,1025]{2,1,0:T(8,128)(2,1)}, u32[]{:S(2)}, u32[]{:S(2)}) %all-to-all-start.1) | async-done | bytes 2099232 | tf_op jit(solution)/shard_map/all_to_all | solution.py:30
  108.4 3.2 %slice.88 = bf16[64,16,1024]{2,1,0:T(8,128)(2,1)} slice(bf16[64,16,1025]{2,1,0:T(8,128)(2,1)} %all-to-all-done.1), slice={[0:64], [0:16], [0:1024]} | slice | bytes 4194304 | tf_op jit(solution)/shard_map/slice | solution.py:35
  111.6 4.2 %reshape_reshape.5 = bf16[8,8,128,128]{3,2,1,0:T(8,128)(2,1)} reshape(bf16[64,16,1024]{2,1,0:T(8,128)(2,1)} %slice.88) | data formatting | bytes 4194304 | tf_op jit(solution)/shard_map/reshape;reshape | solution.py:104
  115.8 128.2 %while.12 = (s32[]{:T(128)}, f32[8,8,128]{2,1,0:T(8,128)S(1)}, f32[8,8,128]{2,1,0:T(8,128)S(1)}, pred[8,8,128]{2,1,0:T(8,128)(4,1)S(1)}, bf16[8,8,128,128]{3,2,1...) while((s32[]{:T(128)}, f32[8,8,128]{2,1,0:T(8,128)S(1)}, f32[8,8,128]{2,1,0:T(8,128)S(1)}, ...), condition=%wide.region_4.5_spmd, body=%wide.region_0.0_spmd.sunk | while | flops 37095552 | bytes 24178844 | solution.py:107
  119.6 10.5 %top_k.18 = (f32[8,128,128]{1,2,0:T(8,128)S(1)}, s32[8,128,128]{1,2,0:T(8,128)}) sort(f32[8,128,128]{1,2,0:T(8,128)S(1)} %copy.114, s32[8,128,128]{1,2,0:T(8,128)S(1)} %iota.23.clone.2), dimensions={2}, to_apply=%region_3.3 | sort | flops 2228224 | bytes 2097152 | tf_op jit(solution)/shard_map/while/body/eval_jaxpr/top_k | solution.py:99
  135.6 10.5 %top_k.18 = (f32[8,128,128]{1,2,0:T(8,128)S(1)}, s32[8,128,128]{1,2,0:T(8,128)}) sort(f32[8,128,128]{1,2,0:T(8,128)S(1)} %copy.114, s32[8,128,128]{1,2,0:T(8,128)S(1)} %iota.23.clone.2), dimensions={2}, to_apply=%region_3.3 | sort | flops 2228224 | bytes 2097152 | tf_op jit(solution)/shard_map/while/body/eval_jaxpr/top_k | solution.py:99
  151.6 10.5 %top_k.18 = (f32[8,128,128]{1,2,0:T(8,128)S(1)}, s32[8,128,128]{1,2,0:T(8,128)}) sort(f32[8,128,128]{1,2,0:T(8,128)S(1)} %copy.114, s32[8,128,128]{1,2,0:T(8,128)S(1)} %iota.23.clone.2), dimensions={2}, to_apply=%region_3.3 | sort | flops 2228224 | bytes 2097152 | tf_op jit(solution)/shard_map/while/body/eval_jaxpr/top_k | solution.py:99
  167.7 10.5 %top_k.18 = (f32[8,128,128]{1,2,0:T(8,128)S(1)}, s32[8,128,128]{1,2,0:T(8,128)}) sort(f32[8,128,128]{1,2,0:T(8,128)S(1)} %copy.114, s32[8,128,128]{1,2,0:T(8,128)S(1)} %iota.23.clone.2), dimensions={2}, to_apply=%region_3.3 | sort | flops 2228224 | bytes 2097152 | tf_op jit(solution)/shard_map/while/body/eval_jaxpr/top_k | solution.py:99
  183.7 10.5 %top_k.18 = (f32[8,128,128]{1,2,0:T(8,128)S(1)}, s32[8,128,128]{1,2,0:T(8,128)}) sort(f32[8,128,128]{1,2,0:T(8,128)S(1)} %copy.114, s32[8,128,128]{1,2,0:T(8,128)S(1)} %iota.23.clone.2), dimensions={2}, to_apply=%region_3.3 | sort | flops 2228224 | bytes 2097152 | tf_op jit(solution)/shard_map/while/body/eval_jaxpr/top_k | solution.py:99
  199.7 10.5 %top_k.18 = (f32[8,128,128]{1,2,0:T(8,128)S(1)}, s32[8,128,128]{1,2,0:T(8,128)}) sort(f32[8,128,128]{1,2,0:T(8,128)S(1)} %copy.114, s32[8,128,128]{1,2,0:T(8,128)S(1)} %iota.23.clone.2), dimensions={2}, to_apply=%region_3.3 | sort | flops 2228224 | bytes 2097152 | tf_op jit(solution)/shard_map/while/body/eval_jaxpr/top_k | solution.py:99
  215.7 10.5 %top_k.18 = (f32[8,128,128]{1,2,0:T(8,128)S(1)}, s32[8,128,128]{1,2,0:T(8,128)}) sort(f32[8,128,128]{1,2,0:T(8,128)S(1)} %copy.114, s32[8,128,128]{1,2,0:T(8,128)S(1)} %iota.23.clone.2), dimensions={2}, to_apply=%region_3.3 | sort | flops 2228224 | bytes 2097152 | tf_op jit(solution)/shard_map/while/body/eval_jaxpr/top_k | solution.py:99
  231.7 10.5 %top_k.18 = (f32[8,128,128]{1,2,0:T(8,128)S(1)}, s32[8,128,128]{1,2,0:T(8,128)}) sort(f32[8,128,128]{1,2,0:T(8,128)S(1)} %copy.114, s32[8,128,128]{1,2,0:T(8,128)S(1)} %iota.23.clone.2), dimensions={2}, to_apply=%region_3.3 | sort | flops 2228224 | bytes 2097152 | tf_op jit(solution)/shard_map/while/body/eval_jaxpr/top_k | solution.py:99
  245.0 4.0 %all-to-all-start.2 = ((f32[4,128,128]{1,2,0:T(8,128)}), f32[4,128,128]{1,2,0:T(8,128)S(1)}, u32[]{:S(2)}, u32[]{:S(2)}) async-start(f32[4,128,128]{1,2,0:T(8,128)} %broadcast_in_dim.111), calls=%async_computation.2 | async-start | bytes 524288 | tf_op jit(solution)/shard_map/all_to_all | solution.py:43
  249.0 5.5 %all-to-all-done.2 = f32[4,128,128]{1,2,0:T(8,128)S(1)} async-done(((f32[4,128,128]{1,2,0:T(8,128)}), f32[4,128,128]{1,2,0:T(8,128)S(1)}, u32[]{:S(2)}, u32[]{:S(2)}) %all-to-all-start.2) | async-done | bytes 262176 | tf_op jit(solution)/shard_map/all_to_all | solution.py:43
  255.6 8.2 %all-to-all-start.3 = ((f32[64,1,1]{2,1,0:T(1,128)}), f32[64,1,1]{2,1,0:T(1,128)S(1)}, u32[]{:S(2)}, u32[]{:S(2)}) async-start(f32[64,1,1]{2,1,0:T(1,128)} %copy.104), calls=%async_computation.3 | async-start | bytes 65536 | tf_op jit(solution)/shard_map/all_to_all | solution.py:149
  264.6 8.6 %all-to-all-done.3 = f32[64,1,1]{2,1,0:T(1,128)S(1)} async-done(((f32[64,1,1]{2,1,0:T(1,128)}), f32[64,1,1]{2,1,0:T(1,128)S(1)}, u32[]{:S(2)}, u32[]{:S(2)}) %all-to-all-start.3) | async-done | bytes 288 | tf_op jit(solution)/shard_map/all_to_all | solution.py:149
  (191 shorter events, 64.3 us)
Async XLA Ops:
  9.3 22.5 %all-to-all-start = ((s32[64,1,17]{2,1,0:T(1,128)}), s32[64,1,17]{2,1,0:T(1,128)S(1)}, u32[]{:S(2)}, u32[]{:S(2)}) async-start(s32[64,1,17]{2,1,0:T(1,128)} %bitcast.9), calls=%async_computation | async-start | bytes 65536 | tf_op jit(solution)/shard_map/all_to_all | solution.py:30
  32.1 7.1 %copy-start = (bf16[2,64,1024]{2,1,0:T(8,128)(2,1)S(1)}, bf16[2,64,1024]{2,1,0:T(8,128)(2,1)}, u32[]{:S(2)}) copy-start(bf16[2,64,1024]{2,1,0:T(8,128)(2,1)} %param.8) | copy-start | bytes 786436
  45.3 5.8 %copy-start.5 = (s32[2,64]{1,0:T(2,128)S(1)}, s32[2,64]{1,0:T(2,128)}, u32[]{:S(2)}) copy-start(s32[2,64]{1,0:T(2,128)} %param.9) | copy-start | bytes 1540
  45.3 6.7 %copy-start.3 = (s32[64,16]{0,1:T(8,128)S(1)}, s32[64,16]{0,1:T(8,128)}, u32[]{:S(2)}) copy-start(s32[64,16]{0,1:T(8,128)} %param.11) | copy-start | bytes 12292
  45.3 7.0 %copy-start.4 = (s32[64,1]{0,1:T(1,128)S(1)}, s32[64,1]{0,1:T(1,128)}, u32[]{:S(2)}) copy-start(s32[64,1]{0,1:T(1,128)} %param.13) | copy-start | bytes 772
  45.3 61.3 %all-to-all-start.1 = ((bf16[64,16,1025]{2,1,0:T(8,128)(2,1)}), bf16[64,16,1025]{2,1,0:T(8,128)(2,1)}, u32[]{:S(2)}, u32[]{:S(2)}) async-start(bf16[64,16,1025]{2,1,0:T(8,128)(2,1)} %pad_maximum_fusion), calls=%async_computation.1 | async-start | bytes 4718592 | tf_op jit(solution)/shard_map/all_to_all | solution.py:30
  51.0 28.9 %all-gather.2.cloned.1.call-start = ((), (), s32[]{:S(2)}) async-start(), calls=%async_computation.4 | async-start | bytes 1474560 | tf_op jit(solution)/shard_map/all_gather | solution.py:21
  81.0 7.0 %slice-start = ((bf16[2,256,1025]{2,1,0:T(8,128)(2,1)}), bf16[2,256,1024]{2,1,0:T(8,128)(2,1)S(1)}, s32[]{:S(2)}) async-start(bf16[2,256,1025]{2,1,0:T(8,128)(2,1)} %all-gather.2.cloned.1.call-done), calls=%async_computation.5 | async-start | bytes 2097152 | tf_op jit(solution)/shard_map/split | solution.py:22
  115.8 3.7 %copy-start.1 = (bf16[8,8,128,128]{3,2,1,0:T(8,128)(2,1)}, bf16[8,8,128,128]{3,2,1,0:T(8,128)(2,1)S(1)}, u32[]{:S(2)}) copy-start(bf16[8,8,128,128]{3,2,1,0:T(8,128)(2,1)S(1)} %get-tuple-element.149) | copy-start | bytes 6291460 | tf_op jit(solution)/shard_map/while
  130.3 1.6 copy-start.2
  131.9 3.7 %copy-start.1 = (bf16[8,8,128,128]{3,2,1,0:T(8,128)(2,1)}, bf16[8,8,128,128]{3,2,1,0:T(8,128)(2,1)S(1)}, u32[]{:S(2)}) copy-start(bf16[8,8,128,128]{3,2,1,0:T(8,128)(2,1)S(1)} %get-tuple-element.149) | copy-start | bytes 6291460 | tf_op jit(solution)/shard_map/while
  146.3 1.6 copy-start.2
  147.9 3.7 %copy-start.1 = (bf16[8,8,128,128]{3,2,1,0:T(8,128)(2,1)}, bf16[8,8,128,128]{3,2,1,0:T(8,128)(2,1)S(1)}, u32[]{:S(2)}) copy-start(bf16[8,8,128,128]{3,2,1,0:T(8,128)(2,1)S(1)} %get-tuple-element.149) | copy-start | bytes 6291460 | tf_op jit(solution)/shard_map/while
  162.3 1.6 copy-start.2
  163.9 3.7 %copy-start.1 = (bf16[8,8,128,128]{3,2,1,0:T(8,128)(2,1)}, bf16[8,8,128,128]{3,2,1,0:T(8,128)(2,1)S(1)}, u32[]{:S(2)}) copy-start(bf16[8,8,128,128]{3,2,1,0:T(8,128)(2,1)S(1)} %get-tuple-element.149) | copy-start | bytes 6291460 | tf_op jit(solution)/shard_map/while
  178.3 1.6 copy-start.2
  179.9 3.7 %copy-start.1 = (bf16[8,8,128,128]{3,2,1,0:T(8,128)(2,1)}, bf16[8,8,128,128]{3,2,1,0:T(8,128)(2,1)S(1)}, u32[]{:S(2)}) copy-start(bf16[8,8,128,128]{3,2,1,0:T(8,128)(2,1)S(1)} %get-tuple-element.149) | copy-start | bytes 6291460 | tf_op jit(solution)/shard_map/while
  194.3 1.6 copy-start.2
  195.9 3.7 %copy-start.1 = (bf16[8,8,128,128]{3,2,1,0:T(8,128)(2,1)}, bf16[8,8,128,128]{3,2,1,0:T(8,128)(2,1)S(1)}, u32[]{:S(2)}) copy-start(bf16[8,8,128,128]{3,2,1,0:T(8,128)(2,1)S(1)} %get-tuple-element.149) | copy-start | bytes 6291460 | tf_op jit(solution)/shard_map/while
  211.9 3.7 %copy-start.1 = (bf16[8,8,128,128]{3,2,1,0:T(8,128)(2,1)}, bf16[8,8,128,128]{3,2,1,0:T(8,128)(2,1)S(1)}, u32[]{:S(2)}) copy-start(bf16[8,8,128,128]{3,2,1,0:T(8,128)(2,1)S(1)} %get-tuple-element.149) | copy-start | bytes 6291460 | tf_op jit(solution)/shard_map/while
  226.3 1.6 copy-start.2
  227.9 3.7 %copy-start.1 = (bf16[8,8,128,128]{3,2,1,0:T(8,128)(2,1)}, bf16[8,8,128,128]{3,2,1,0:T(8,128)(2,1)S(1)}, u32[]{:S(2)}) copy-start(bf16[8,8,128,128]{3,2,1,0:T(8,128)(2,1)S(1)} %get-tuple-element.149) | copy-start | bytes 6291460 | tf_op jit(solution)/shard_map/while
  245.0 9.5 %all-to-all-start.2 = ((f32[4,128,128]{1,2,0:T(8,128)}), f32[4,128,128]{1,2,0:T(8,128)S(1)}, u32[]{:S(2)}, u32[]{:S(2)}) async-start(f32[4,128,128]{1,2,0:T(8,128)} %broadcast_in_dim.111), calls=%async_computation.2 | async-start | bytes 524288 | tf_op jit(solution)/shard_map/all_to_all | solution.py:43
  255.6 17.6 %all-to-all-start.3 = ((f32[64,1,1]{2,1,0:T(1,128)}), f32[64,1,1]{2,1,0:T(1,128)S(1)}, u32[]{:S(2)}, u32[]{:S(2)}) async-start(f32[64,1,1]{2,1,0:T(1,128)} %copy.104), calls=%async_computation.3 | async-start | bytes 65536 | tf_op jit(solution)/shard_map/all_to_all | solution.py:149
  (2 other events, 3.2 us)
Sparse Core Ops, SparseCore 0:
  53.6 26.2 all-gather.1
where the time goes:
time: 283 us; the launch traced here: 281 us
  other arithmetic  110 us (39%)
  waiting for transfers between devices  58.2 us (21%)
  local copies, waits for them, and re-layouts  56 us (20%)
  starting transfers between devices  31.1 us (11%)
  between operations  14.4 us (5%)
  matrix products  11.3 us (4%)
    top_k x8, other arithmetic, one_group(): lowest = -lax.top_k(-dist, 2)[0]  83.7 us
    all_gather x1, waiting for transfers between devices, in_one_piece(): out = lax.all_gather(both, axis, axis=dim, tiled=True)  26.6 us
    all_to_all x2, starting transfers between devices, in_one_piece_2(): lax.all_to_all(both, axis, split_axis=split_dim, concat_axis=concat_dim,...  18.9 us
    all_to_all x2, waiting for transfers between devices, in_one_piece_2(): lax.all_to_all(both, axis, split_axis=split_dim, concat_axis=concat_dim,...  17.6 us
    dot_general x8, matrix products, one_group(): jnp.einsum('pqd,pcd->pqc', query_part, cand_part, preferred_element_type=...  11.3 us
    while x40, local copies, waits for them, and re-layouts  9.66 us
    reduce_sum x8, other arithmetic, one_group(): cnorm = jnp.sum(cwide * cwide, axis=2)  9.3 us
    all_to_all x1, waiting for transfers between devices, on_device(): lax.all_to_all(score, 'img', split_axis=0, concat_axis=0, tiled=True)  8.55 us
  transfers between devices with their start and end apart: 5, of which 5 were waited for; matrix products, arithmetic and copies ran while one was open for 8% of the time, Pallas kernels for 0%

commit v1 on v0

v1 whole, which is shorter than its diff:
```python
import functools

import jax
import jax.numpy as jnp
from jax import lax
from jax.experimental import pallas as pl
from jax.experimental.pallas import tpu as pltpu
from jax.sharding import PartitionSpec as P

DESC = 128
KP = 8

dead_entry = 16384.0
cut = 1.0e6
f32 = jnp.float32
bf16 = jnp.bfloat16


def vmem():
    return pl.BlockSpec(memory_space=pltpu.VMEM)


def smem():
    return pl.BlockSpec(memory_space=pltpu.SMEM)


def pick_queries(rep, cells, cells_ref, first_ref, at_ref, own, one, two, three, out):
    me = at_ref[1]
    pairs = first_ref.shape[0]
    share = own.shape[0] // 2
    part = out.shape[1]

    def step(p, _):
        base = (first_ref[p, 0] & 1) * share
        for u in range(part):
            cell = cells_ref[p, me * part + u]
            row = base + cell % share
            back = (me - cell // share + rep) % rep
            tile = jnp.where(
                back < 2,
                jnp.where(back == 0, own[row], one[row]),
                jnp.where(back == 2, two[row], three[row]),
            )
            out[p, u] = tile
        return 0

    lax.fori_loop(0, pairs, step, 0)


def gather_candidates(rep, at_ref, meta, own, one, two, three, out, norms, table, cnorm):
    me = at_ref[1]
    count = own.shape[0]
    width = count + 1
    group = 4
    block = 16
    for back, source in enumerate((own, one, two, three)):
        base = ((me - back + rep) % rep) * width

        def fill(c, _, source=source, base=base):
            x = source[pl.ds(c * block, block)].astype(f32)
            table[pl.ds(base + c * block, block)] = x
            sums = jnp.sum(x * x, axis=2, keepdims=True)
            cnorm[pl.ds(base + c * block, block)] = jnp.broadcast_to(sums, x.shape)
            return 0

        lax.fori_loop(0, count // block, fill, 0)
        table[base + count] = jnp.full((KP, DESC), dead_entry, f32)
        cnorm[base + count] = jnp.full((KP, DESC), dead_entry * dead_entry * DESC, f32)

    slots = norms.shape[1] // KP // rep
    lane_group = lax.broadcasted_iota(jnp.int32, (KP, DESC), 1) // (DESC // group)

    def quad(g, _):
        for q in range(rep):
            for s in range(0, slots, 2):
                t = q * slots + s
                where = [
                    [meta[(g * group + i) * rep + q, s + h] for h in range(2)] for i in range(group)
                ]
                for i in range(group):
                    both = jnp.concatenate([table[where[i][0]], table[where[i][1]]], axis=0)
                    out[g, t * KP : (t + 2) * KP, i * DESC : (i + 1) * DESC] = both.astype(bf16)
                for h in range(2):
                    low = jnp.where(lane_group == 0, cnorm[where[0][h]], cnorm[where[1][h]])
                    high = jnp.where(lane_group == 2, cnorm[where[2][h]], cnorm[where[3][h]])
                    norms[g, (t + h) * KP : (t + h + 1) * KP, :] = jnp.where(
                        lane_group < 2, low, high
                    )
        return 0

    lax.fori_loop(0, out.shape[0], quad, 0)


def keep_two(left, right):
    low = jnp.minimum(left[0], right[0])
    high = jnp.minimum(jnp.maximum(left[0], right[0]), jnp.minimum(left[1], right[1]))
    return low, high


def match(rep, at_ref, meta, queries, cands, norms, out):
    group = 4
    size = DESC // group
    rows = cands.shape[1]
    row_ids = lax.broadcasted_iota(jnp.int32, (DESC, DESC), 0)
    lane_ids = lax.broadcasted_iota(jnp.int32, (DESC, DESC), 1)
    diagonal = row_ids == lane_ids
    lanes = lax.broadcasted_iota(jnp.int32, (KP, DESC), 1)
    lane_group = lanes // size

    def quad(g, sums):
        q = queries[pl.ds(g * group, group)].astype(f32).reshape(DESC, DESC)
        square = jnp.sum(q * q, axis=1, keepdims=True)
        spread = jnp.where(diagonal, square, 0.0).reshape(DESC // KP, KP, DESC)
        qnorm = jnp.sum(jnp.sum(spread, axis=0), axis=0, keepdims=True)
        qnorm = jnp.broadcast_to(qnorm, (KP, DESC))
        twice = q * -2.0
        right = jnp.concatenate(
            [
                jnp.where(row_ids // size == i, twice, 0.0).astype(bf16)
                for i in range(group)
            ],
            axis=1,
        )
        inner = lax.dot_general(
            cands[g], right, (((1,), (1,)), ((), ())), preferred_element_type=f32
        )
        dist = (inner + norms[g]).reshape(rows // KP, KP, DESC)
        sides = [(dist[k], dist[k + 1]) for k in range(0, rows // KP, 2)]
        sides = [(jnp.minimum(a, b), jnp.maximum(a, b)) for a, b in sides]
        while len(sides) > 1:
            sides = [keep_two(sides[k], sides[k + 1]) for k in range(0, len(sides), 2)]
        low, high = sides[0]
        for turn in (4, 2, 1):
            low, high = keep_two(
                (low, high), (pltpu.roll(low, turn, 0), pltpu.roll(high, turn, 0))
            )
        live = qnorm < cut
        best = jnp.where(live, low + qnorm, 0.0)
        runner = jnp.where(live, high + qnorm, 0.0)
        margin = (runner - best) / (runner + 1.0)
        totals, seconds = [], []
        for i in range(group):
            row = (g * group + i) * rep
            total = meta[row, 16]
            for r in range(1, rep):
                total = total + meta[row + r, 16]
            totals.append(total.astype(f32))
            seconds.append(meta[row, 17])

        def per_group(values):
            return jnp.where(
                lane_group < 2,
                jnp.where(lane_group == 0, values[0], values[1]),
                jnp.where(lane_group == 2, values[2], values[3]),
            )

        share = margin / per_group(totals)
        second = per_group(seconds)
        for i in range(group):
            left = best if i == 0 else pltpu.roll(best, DESC - size * i, 1)
            at = (size - size * i) % DESC
            other = runner if at == 0 else pltpu.roll(runner, at, 1)
            line = jnp.where(
                lanes < size, left, jnp.where(lanes < 2 * size, other, totals[i])
            )
            out[g * group + i] = line[:rep]
        return (
            sums[0] + jnp.where(second == 0, share, 0.0),
            sums[1] + jnp.where(second == 0, 0.0, share),
        )

    zero = jnp.zeros((KP, DESC), f32)
    sums = lax.fori_loop(0, cands.shape[0], quad, (zero, zero))
    here = at_ref[0]
    parts = [jnp.sum(part[:1], axis=1, keepdims=True) for part in sums]
    line = out[here]
    ids = lanes[:rep]
    out[here] = jnp.where(
        ids < 3 * size, line, jnp.where(ids < 3 * size + size // 2, parts[0], parts[1])
    )


def finish(rep, at_ref, shares, first, matches, scores):
    size = DESC // rep
    here = at_ref[0]
    pairs = matches.shape[0]
    lane_group = lax.broadcasted_iota(jnp.int32, (pairs, DESC), 1) // size
    best = jnp.zeros((pairs, DESC), f32)
    runner = jnp.zeros((pairs, DESC), f32)
    for r in range(rep):
        part = shares[:, r, :]
        left = part if r == 0 else pltpu.roll(part, size * r, 1)
        at = (size * r - size) % DESC
        other = part if at == 0 else pltpu.roll(part, at, 1)
        best = jnp.where(lane_group == r, left, best)
        runner = jnp.where(lane_group == r, other, runner)
    matches[:, 0, :] = best
    matches[:, 1, :] = runner
    total = shares[:, 0, 2 * size : 2 * size + 1]
    score = jnp.sum((runner - best) / (runner + 1.0), axis=1, keepdims=True) / total
    which = first[:, :1]
    mine = shares[here]
    for b in range(2):
        own_part = jnp.sum(jnp.where(which == b, score, 0.0))
        at = 3 * size + b * (size // 2)
        scores[b] = own_part + jnp.sum(mine[:, at : at + 1])


def on_device(descriptors, cell_counts, pair_images, query_cells, cand_cells, cand_counts):
    img_dev, share, width = descriptors.shape
    peers = lax.axis_size("img")
    rep = lax.axis_size("rep")
    me = lax.axis_index("rep").astype(jnp.int32)
    at = jnp.stack([lax.axis_index("img").astype(jnp.int32), me])
    slots = cand_cells.shape[2]
    part = query_cells.shape[1] // rep
    cells = img_dev * share

    slot_ids = jnp.arange(KP, dtype=jnp.int32)
    live = slot_ids[None, :] < cell_counts.reshape(cells)[:, None]
    own = jnp.where(live[:, :, None], descriptors.reshape(cells, KP, DESC), bf16(dead_entry))

    def turned(by):
        return lax.ppermute(own, "rep", [(r, (r + by) % rep) for r in range(rep)])

    one, three, two = turned(1), turned(3), turned(2)

    first = pair_images[:, 0] % img_dev
    second = pair_images[:, 1] % img_dev
    rows = second[:, None] * share + cand_cells[:, 0, :] % share
    alive = jnp.arange(slots, dtype=jnp.int32)[None, :] < cand_counts
    rows = jnp.where(alive, rows, cells) + me * (cells + 1)
    local = first[:, None] * share + query_cells - me * share
    inside = (query_cells >= me * share) & (query_cells < (me + 1) * share)
    local = jnp.where(inside, local, -1)
    hits = local[:, :, None] == jnp.arange(cells, dtype=jnp.int32)[None, None, :]
    partial = jnp.sum(jnp.where(hits, cell_counts.reshape(cells)[None, None, :], 0), axis=(1, 2))
    note = jnp.concatenate([rows, partial[:, None], second[:, None]], axis=1)
    note = jnp.pad(note, ((0, 0), (0, DESC - note.shape[1])))
    note = jnp.broadcast_to(note[:, None, :], (peers, rep, DESC)).reshape(peers * rep, 1, DESC)
    meta = lax.all_to_all(note, ("img", "rep"), split_axis=0, concat_axis=0, tiled=True)
    meta = meta.reshape(peers * rep, DESC)

    message = pl.pallas_call(
        functools.partial(pick_queries, rep, cells),
        out_shape=jax.ShapeDtypeStruct((peers, part, KP, DESC), bf16),
        in_specs=[smem(), smem(), smem(), vmem(), vmem(), vmem(), vmem()],
        out_specs=vmem(),
        name="pick_queries",
    )(query_cells, pair_images, at, own, one, two, three)
    queries = lax.all_to_all(
        message.reshape(peers, part * KP, DESC), "img", split_axis=0, concat_axis=0, tiled=True
    )

    quads = peers // 4
    lines = rep * slots * KP
    cands, norms = pl.pallas_call(
        functools.partial(gather_candidates, rep),
        out_shape=(
            jax.ShapeDtypeStruct((quads, lines, 4 * DESC), bf16),
            jax.ShapeDtypeStruct((quads, lines, DESC), f32),
        ),
        in_specs=[smem(), smem(), vmem(), vmem(), vmem(), vmem()],
        out_specs=(vmem(), vmem()),
        scratch_shapes=[
            pltpu.VMEM((rep * (cells + 1), KP, DESC), f32),
            pltpu.VMEM((rep * (cells + 1), KP, DESC), f32),
        ],
        name="gather_candidates",
    )(at, meta, own, one, two, three)

    shares = pl.pallas_call(
        functools.partial(match, rep),
        out_shape=jax.ShapeDtypeStruct((peers, rep, DESC), f32),
        in_specs=[smem(), smem(), vmem(), vmem(), vmem()],
        out_specs=vmem(),
        name="match",
    )(at, meta, queries, cands, norms)
    shares = lax.all_to_all(
        shares.reshape(peers * rep, 1, DESC), ("img", "rep"), split_axis=0, concat_axis=0, tiled=True
    ).reshape(peers, rep, DESC)

    return pl.pallas_call(
        functools.partial(finish, rep),
        out_shape=(
            jax.ShapeDtypeStruct((peers, 2, DESC), f32),
            jax.ShapeDtypeStruct((img_dev,), f32),
        ),
        in_specs=[smem(), vmem(), vmem()],
        out_specs=(vmem(), smem()),
        name="finish",
    )(at, shares, jnp.broadcast_to(first[:, None], (peers, DESC)))


def solution(mesh):
    in_specs = (
        P("img", "rep", None),
        P("img", "rep"),
        P("img", None),
        P("img", None),
        P("img", "rep", None),
        P("img", "rep"),
    )
    out_specs = (P("img", None, None), P("img"))
    return jax.shard_map(
        on_device, mesh=mesh, in_specs=in_specs, out_specs=out_specs, check_vma=False
    )
```

time: 283 us -> 106 us (0.37)
  other arithmetic: 110 us -> 4.52 us
  waiting for transfers between devices: 58.2 us -> 2.7 us
  local copies, waits for them, and re-layouts: 56 us -> 8.35 us
  Pallas kernels: 0 us -> 36.2 us
  blocking collectives: 0 us -> 24.1 us
  between operations: 14.4 us -> 0.74 us
  matrix products: 11.3 us -> 0 us
    top_k x8 -> x0, other arithmetic: 83.7 us -> none  [one_group(): lowest = -lax.top_k(-dist, 2)[0]]
    pallas_call x0 -> x4, Pallas kernels: none -> 36.2 us  [the longest x1 16.1 us: on_device(): pl.pallas_call(functools.partial(gather_candidates, rep), out_shape=(jax....]
    all_to_all x4 -> x2, waiting for transfers between devices: 31.6 us -> 2.69 us  [the longest x1 1.62 us: on_device(): lax.all_to_all(message.reshape(peers, part * KP, DESC), 'img', split_axis...]
    all_gather x1 -> x0, waiting for transfers between devices: 26.6 us -> none  [in_one_piece(): out = lax.all_gather(both, axis, axis=dim, tiled=True)]
    gather x9 -> x0, local copies, waits for them, and re-layouts: 24.1 us -> none  [the longest x3 6.96 us: on_device(): jnp.take(whole_counts.reshape(img_dev * cells), query_rows)]
    all_to_all x0 -> x1, blocking collectives: none -> 24.1 us  [on_device(): lax.all_to_all(shares.reshape(peers * rep, 1, DESC), ('img', 'rep'), spli...]
    dot_general x8 -> x0, matrix products: 11.3 us -> none  [one_group(): jnp.einsum('pqd,pcd->pqc', query_part, cand_part, preferred_element_type=...]
    while x40 -> x0, local copies, waits for them, and re-layouts: 9.66 us -> none
  transfers between devices with their start and end apart: 5 -> 5, of which waited for: 5 -> 2; matrix products, arithmetic and copies ran while one was open for 8% -> 7% of each run, Pallas kernels for 0% -> 22%
where the time goes in v1:
time: 106 us
  Pallas kernels  36.2 us (34%)
  starting transfers between devices  29.1 us (27%)
  blocking collectives  24.1 us (23%)
  local copies, waits for them, and re-layouts  8.35 us (8%)
  other arithmetic  4.52 us (4%)
  waiting for transfers between devices  2.7 us (3%)
    all_to_all x1, blocking collectives, on_device(): lax.all_to_all(shares.reshape(peers * rep, 1, DESC), ('img', 'rep'), spli...  24.1 us
    pallas_call x1, Pallas kernels, on_device(): pl.pallas_call(functools.partial(gather_candidates, rep), out_shape=(jax....  16.1 us
    all_to_all x1, starting transfers between devices, on_device(): lax.all_to_all(note, ('img', 'rep'), split_axis=0, concat_axis=0, tiled=T...  13.2 us
    pallas_call x1, Pallas kernels, on_device(): pl.pallas_call(functools.partial(match, rep), out_shape=jax.ShapeDtypeStr...  11.5 us
    all_to_all x1, starting transfers between devices, on_device(): lax.all_to_all(message.reshape(peers, part * KP, DESC), 'img', split_axis...  10.2 us
    pallas_call x1, Pallas kernels, on_device(): pl.pallas_call(functools.partial(pick_queries, rep, cells), out_shape=jax...  6.74 us
    unnamed x16, local copies, waits for them, and re-layouts  6.14 us
    ppermute x3, starting transfers between devices, turned(): return lax.ppermute(own, 'rep', [(r, (r + by) % rep) for r in range(rep)])  5.71 us
  transfers between devices with their start and end apart: 5, of which 2 were waited for; matrix products, arithmetic and copies ran while one was open for 7% of the time, Pallas kernels for 22%

profile of v1, /device:TPU:1, one launch (start us, length us, event | category | flops | bytes accessed | tf_op | source)
XLA Modules:
  0.0 105.7 jit_solution(11001235669525703581)
XLA Ops:
  0.6 0.8 broadcast_in_dim.60
  1.4 1.0 copy.23
  2.7 2.1 %collective-permute-start = (bf16[128,8,128]{2,1,0:T(8,128)(2,1)S(1)}, bf16[128,8,128]{2,1,0:T(8,128)(2,1)S(1)}, u32[]{:S(2)}, u32[]{:S(2)}) collective-permute-start(bf16[128,8,128]{2,1,0:T(8,128)(2,1)S(1)} %bitcast_select_fusion.own), channel_id=1, source_target_pairs={{0,1},{1,2},{2,3},{3,0},{4,5},{5,6},{6,7},{7,4},{8,9},{9,10},{10,1... | collective-permute-start | bytes 786440 | tf_op jit(solution)/shard_map/ppermute | solution.py:224
  4.8 2.5 %collective-permute-start.1 = (bf16[128,8,128]{2,1,0:T(8,128)(2,1)S(1)}, bf16[128,8,128]{2,1,0:T(8,128)(2,1)S(1)}, u32[]{:S(2)}, u32[]{:S(2)}) collective-permute-start(bf16[128,8,128]{2,1,0:T(8,128)(2,1)S(1)} %bitcast_select_fusion.own), channel_id=1, source_target_pairs={{0,2},{1,3},{2,0},{3,1},{4,6},{5,7},{6,4},{7,5},{8,10},{9,11},{10,... | collective-permute-start | bytes 786440 | tf_op jit(solution)/shard_map/ppermute | solution.py:224
  7.3 1.2 %collective-permute-start.2 = (bf16[128,8,128]{2,1,0:T(8,128)(2,1)S(1)}, bf16[128,8,128]{2,1,0:T(8,128)(2,1)S(1)}, u32[]{:S(2)}, u32[]{:S(2)}) collective-permute-start(bf16[128,8,128]{2,1,0:T(8,128)(2,1)S(1)} %bitcast_select_fusion.own), channel_id=1, source_target_pairs={{0,3},{1,0},{2,1},{3,2},{4,7},{5,4},{6,5},{7,6},{8,11},{9,8},{10,9... | collective-permute-start | bytes 786440 | tf_op jit(solution)/shard_map/ppermute | solution.py:224
  8.4 0.8 multiply_bitcast_fusion
  9.2 0.7 subtract_select_fusion
  10.0 1.4 %select_reduce_fusion = s32[64]{0:T(128)S(1)} fusion(s32[128]{0:T(128)S(1)} %broadcast_in_dim.60, s32[64,16]{1,0:T(8,128)S(1)} %copy.17), kind=kLoop, calls=%fused_computation | loop fusion | flops 393152 | bytes 4864 | tf_op jit(solution)/shard_map/reduce_sum | solution.py:237
  11.4 0.7 fusion.3
  12.2 0.7 broadcast_in_dim.64
  12.9 13.2 %all-to-all-start = ((s32[256,1,128]{2,1,0:T(1,128)}), s32[256,1,128]{2,1,0:T(1,128)S(1)}, u32[]{:S(2)}, u32[]{:S(2)}) async-start(s32[256,1,128]{2,1,0:T(1,128)} %bitcast.7), calls=%async_computation | async-start | bytes 262144 | tf_op jit(solution)/shard_map/all_to_all | solution.py:241
  26.1 1.4 %copy.19.cells_ref = s32[64,16]{1,0:T(8,128)} copy(s32[64,16]{0,1:T(8,128)} %param.9) | data formatting | bytes 8192 | tf_op args[3]
  27.5 1.4 %copy.20.first_ref = s32[64,2]{1,0:T(8,128)} copy(s32[64,2]{0,1:T(2,128)} %param.8) | data formatting | bytes 1024 | tf_op args[2]
  30.4 0.7 copy-done.5
  31.0 6.7 %pick_queries.1 = bf16[64,4,8,128]{3,2,1,0:T(8,128)(2,1)} custom-call(s32[64,16]{1,0:T(8,128)} %copy.19.cells_ref, s32[64,2]{1,0:T(8,128)} %copy.20.first_ref, s32[2]{0:T(128)} %pad_add_fusion.1.at_ref, bf16[128,8,128]{2,1,0:T(8,128)(2,1)} %copy-done, bf16[128,8,128]{2,1,0:T(8,128)(2,1)} %copy-done.3, bf16[128,8,128]{2,1,0:T(8,128)(2,1)} %copy-done.4, ...), custom_call_target="tpu_custom_call" | custom-call | tf_op jit(solution)/shard_map/pick_queries/pallas_call | solution.py:244
  37.8 1.1 %all-to-all-done = s32[256,1,128]{2,1,0:T(1,128)S(1)} async-done(((s32[256,1,128]{2,1,0:T(1,128)}), s32[256,1,128]{2,1,0:T(1,128)S(1)}, u32[]{:S(2)}, u32[]{:S(2)}) %all-to-all-start) | async-done | bytes 131104 | tf_op jit(solution)/shard_map/all_to_all | solution.py:241
  38.9 10.2 %all-to-all-start.1 = ((bf16[64,32,128]{2,1,0:T(8,128)(2,1)}), bf16[64,32,128]{2,1,0:T(8,128)(2,1)S(1)}, u32[]{:S(2)}, u32[]{:S(2)}) async-start(bf16[64,32,128]{2,1,0:T(8,128)(2,1)} %bitcast.24), calls=%async_computation.1 | async-start | bytes 1048576 | tf_op jit(solution)/shard_map/all_to_all | solution.py:251
  49.1 16.1 %gather_candidates.1 = (bf16[16,512,512]{2,1,0:T(8,128)(2,1)}, f32[16,512,128]{2,1,0:T(8,128)}) custom-call(s32[2]{0:T(128)} %pad_add_fusion.1.at_ref, s32[256,128]{1,0:T(8,128)} %bitcast.25, bf16[128,8,128]{2,1,0:T(8,128)(2,1)} %copy-done, bf16[128,8,128]{2,1,0:T(8,128)(2,1)} %copy-done.3, bf16[128,8,128]{2,1,0:T(8,128)(2,1)} %copy-done.4, ...), custom_call_target="tpu_custom_call" | custom-call | tf_op jit(solution)/shard_map/gather_candidates/pallas_call | solution.py:257
  65.1 1.6 %all-to-all-done.1.queries = bf16[64,32,128]{2,1,0:T(8,128)(2,1)S(1)} async-done(((bf16[64,32,128]{2,1,0:T(8,128)(2,1)}), bf16[64,32,128]{2,1,0:T(8,128)(2,1)S(1)}, u32[]{:S(2)}, u32[]{:S(2)}) %all-to-all-start.1) | async-done | bytes 524320 | tf_op jit(solution)/shard_map/all_to_all | solution.py:251
  66.7 0.8 copy-done.1
  67.6 11.5 %match.1 = f32[64,4,128]{2,1,0:T(4,128)} custom-call(s32[2]{0:T(128)} %pad_add_fusion.1.at_ref, s32[256,128]{1,0:T(8,128)} %bitcast.26, bf16[64,32,128]{2,1,0:T(8,128)(2,1)} %copy-done.1, bf16[16,512,512]{2,1,0:T(8,128)(2,1)} %get-tuple-element.4.cands, f32[16,512,128]{2,1,0:T(8,128)} %get-tuple-element.5.norms), custom_call_target="tpu_custom_call" | custom-call | tf_op jit(solution)/shard_map/match/pallas_call | solution.py:272
  79.1 24.1 %all_to_all.15 = f32[256,1,128]{2,1,0:T(1,128)} all-to-all(f32[256,1,128]{2,1,0:T(1,128)} %bitcast.28), channel_id=1, replica_groups=mesh['img'=64,'rep'=4] {'img','rep'}, dimensions={0} | all-to-all | bytes 262144 | tf_op jit(solution)/shard_map/all_to_all | solution.py:279
  103.2 0.7 broadcast_in_dim.68.first
  103.9 1.8 %finish.1 = (f32[64,2,128]{2,1,0:T(2,128)}, f32[2]{0:T(128)}) custom-call(s32[2]{0:T(128)} %pad_add_fusion.1.at_ref, f32[64,4,128]{2,1,0:T(4,128)} %bitcast.27, s32[64,128]{1,0:T(8,128)} %broadcast_in_dim.68.first), custom_call_target="tpu_custom_call" | custom-call | tf_op jit(solution)/shard_map/finish/pallas_call | solution.py:283
  (20 shorter events, 1.9 us)
Async XLA Ops:
  2.7 26.9 %copy-start = (bf16[128,8,128]{2,1,0:T(8,128)(2,1)}, bf16[128,8,128]{2,1,0:T(8,128)(2,1)S(1)}, u32[]{:S(2)}) copy-start(bf16[128,8,128]{2,1,0:T(8,128)(2,1)S(1)} %bitcast_select_fusion.own) | copy-start | bytes 786436
  2.7 26.8 %collective-permute-start = (bf16[128,8,128]{2,1,0:T(8,128)(2,1)S(1)}, bf16[128,8,128]{2,1,0:T(8,128)(2,1)S(1)}, u32[]{:S(2)}, u32[]{:S(2)}) collective-permute-start(bf16[128,8,128]{2,1,0:T(8,128)(2,1)S(1)} %bitcast_select_fusion.own), channel_id=1, source_target_pairs={{0,1},{1,2},{2,3},{3,0},{4,5},{5,6},{6,7},{7,4},{8,9},{9,10},{10,1... | collective-permute-start | bytes 786440 | tf_op jit(solution)/shard_map/ppermute | solution.py:224
  4.8 24.7 %collective-permute-start.1 = (bf16[128,8,128]{2,1,0:T(8,128)(2,1)S(1)}, bf16[128,8,128]{2,1,0:T(8,128)(2,1)S(1)}, u32[]{:S(2)}, u32[]{:S(2)}) collective-permute-start(bf16[128,8,128]{2,1,0:T(8,128)(2,1)S(1)} %bitcast_select_fusion.own), channel_id=1, source_target_pairs={{0,2},{1,3},{2,0},{3,1},{4,6},{5,7},{6,4},{7,5},{8,10},{9,11},{10,... | collective-permute-start | bytes 786440 | tf_op jit(solution)/shard_map/ppermute | solution.py:224
  7.3 22.3 %collective-permute-start.2 = (bf16[128,8,128]{2,1,0:T(8,128)(2,1)S(1)}, bf16[128,8,128]{2,1,0:T(8,128)(2,1)S(1)}, u32[]{:S(2)}, u32[]{:S(2)}) collective-permute-start(bf16[128,8,128]{2,1,0:T(8,128)(2,1)S(1)} %bitcast_select_fusion.own), channel_id=1, source_target_pairs={{0,3},{1,0},{2,1},{3,2},{4,7},{5,4},{6,5},{7,6},{8,11},{9,8},{10,9... | collective-permute-start | bytes 786440 | tf_op jit(solution)/shard_map/ppermute | solution.py:224
  12.9 26.0 %all-to-all-start = ((s32[256,1,128]{2,1,0:T(1,128)}), s32[256,1,128]{2,1,0:T(1,128)S(1)}, u32[]{:S(2)}, u32[]{:S(2)}) async-start(s32[256,1,128]{2,1,0:T(1,128)} %bitcast.7), calls=%async_computation | async-start | bytes 262144 | tf_op jit(solution)/shard_map/all_to_all | solution.py:241
  29.5 0.7 copy-start.3
  29.6 0.8 copy-start.4
  30.4 0.7 copy-start.5
  38.9 10.2 %copy-start.2 = (s32[256,1,128]{2,1,0:T(1,128)}, s32[256,1,128]{2,1,0:T(1,128)S(1)}, u32[]{:S(2)}) copy-start(s32[256,1,128]{2,1,0:T(1,128)S(1)} %all-to-all-done) | copy-start | bytes 393220
  38.9 27.9 %all-to-all-start.1 = ((bf16[64,32,128]{2,1,0:T(8,128)(2,1)}), bf16[64,32,128]{2,1,0:T(8,128)(2,1)S(1)}, u32[]{:S(2)}, u32[]{:S(2)}) async-start(bf16[64,32,128]{2,1,0:T(8,128)(2,1)} %bitcast.24), calls=%async_computation.1 | async-start | bytes 1048576 | tf_op jit(solution)/shard_map/all_to_all | solution.py:251
  66.7 0.8 copy-start.1
